TPU v7x, 256 devices: a 2x2x32 block of a 4x8x32 slice. The times are simulated.
256 devices in a mesh: band: 4 (over y, x), row: 64 (over z, core).
Axes of the slice: x: 2, y: 2, z: 32, core: 2. Of those that a mesh axis runs over, the one named last changes fastest.
The devices are a block of a 4x8x32 slice.
Arguments:
- shot_traces: bfloat16 [131072, 4096], P(('band', 'row')), parts along dimension 0, may hold values from -6 to 6
- source_cell: int32 [131072], P(('band', 'row')), parts along dimension 0, may hold values from 0 to 127
- receiver_cell: int32 [131072], P(('band', 'row')), parts along dimension 0, may hold values from 0 to 127
- band_order: int32 [512], P('band'), parts along dimension 0, may hold values from 0 to 127, each once
Outputs:
- next_grid: float32 [512, 2, 128, 128], P(('band', 'row')), parts along dimension 0
There are 4 independent parts, one for each index of `band`. A program takes and returns all parts, laid end to end along the dimension named above; each array names one. Nothing has to cross between parts.
Inputs may be any that keep to these rules, and one draw needn't show every extreme that they name: `band_order`: a permutation of 0 to 127.
All inputs are finite; a program needn't handle non-finite values.
Results may differ from a plain program's by a relative error of at most 0.0037.
Values may be sent and summed in bfloat16 or wider, within the bound.
A program may use at most 64 MiB of HBM per device.

v0:
```python
import math
import jax
import jax.numpy as jnp
from jax import lax
from jax.sharding import PartitionSpec as P

FLO = 64
SC = 128
RC = 128


def local(shot_traces, source_cell, receiver_cell, band_order):
    samples_count = shot_traces.shape[1]
    band_size = band_order.shape[0]
    local_traces = shot_traces.shape[0]
    bins = FLO + band_order
    samples = jnp.arange(samples_count, dtype=jnp.int32)
    phase = samples[:, None] * bins[None, :] % samples_count
    angle = 2.0 * math.pi * phase.astype(jnp.float32) / samples_count
    scale = 1.0 / math.sqrt(samples_count)
    table = jnp.concatenate([jnp.cos(angle) * scale, -jnp.sin(angle) * scale], axis=1).astype(
        jnp.bfloat16
    )
    spectra = jnp.dot(shot_traces, table, preferred_element_type=jnp.float32).astype(jnp.bfloat16)
    spectra = spectra.reshape(local_traces, 2, band_size)
    source_range = jnp.arange(SC, dtype=jnp.float32)
    receiver_range = jnp.arange(RC, dtype=jnp.float32)
    cells = jnp.stack([source_cell, receiver_cell], axis=1).astype(jnp.bfloat16)
    cells = jnp.broadcast_to(cells[:, :, None], (local_traces, 2, band_size))
    packed = jnp.concatenate([spectra, cells], axis=1)
    moved = lax.all_to_all(packed, "row", split_axis=2, concat_axis=0, tiled=True)
    received = moved[:, 0:2, :]
    source_value = moved[:, 2, 0].astype(jnp.float32)
    receiver_value = moved[:, 3, 0].astype(jnp.float32)
    source_hot = (source_value[:, None] == source_range[None, :]).astype(jnp.bfloat16)
    receiver_hot = (receiver_value[:, None] == receiver_range[None, :]).astype(jnp.bfloat16)
    counts = jnp.einsum("ts,tr->sr", source_hot, receiver_hot, preferred_element_type=jnp.float32)
    weighted = received[:, :, :, None] * receiver_hot[:, None, None, :]
    stack = jnp.einsum("ts,tcfr->fcsr", source_hot, weighted, preferred_element_type=jnp.float32)
    next_grid = stack / jnp.maximum(counts, 1.0)[None, None, :, :]
    return next_grid


def solution(mesh):
    placed = (P(("band", "row"), None), P(("band", "row")), P(("band", "row")), P("band"))
    return jax.shard_map(
        local,
        mesh=mesh,
        in_specs=placed,
        out_specs=P(("band", "row"), None, None, None),
        check_vma=False,
    )
```

profile of v0, /device:TPU:44, one launch (start us, length us, event | category | flops | bytes accessed | tf_op | source)
XLA Modules:
  0.0 156.9 jit_solution(13117734031525655496)
XLA Ops:
  0.0 0.7 broadcast_add_fusion
  0.7 0.7 convert.18
  1.4 0.7 convert.19
  2.0 8.6 %multiply_convert_fusion.1 = (bf16[4096,128]{1,0:T(8,128)(2,1)S(1)}, bf16[4096,128]{1,0:T(8,128)(2,1)S(1)}) fusion(s32[128]{0:T(128)S(1)} %broadcast_add_fusion), kind=kLoop, calls=%fused_computation.24 | loop fusion | flops 9961472 | bytes 2097664 | tf_op jit(solution)/shard_map/convert.6
  10.7 3.5 %fusion.23 = bf16[256,512]{1,0:T(8,128)(2,1)S(1)} fusion(bf16[512,4096]{1,0:T(8,128)(2,1)} %param.4, bf16[4096,128]{1,0:T(8,128)(2,1)S(1)} %get-tuple-element.8, bf16[4096,128]{1,0:T(8,128)(2,1)S(1)} %get-tuple-element.7), kind=kOutput, calls=%fused_computation.28 | convolution fusion | flops 1078067200 | bytes 6553600 | tf_op jit(solution)/shard_map/dot_general | solution.py:24
  14.2 0.3 copy.10
  14.5 0.1 broadcast_in_dim.2
  14.6 0.5 pad_maximum_fusion
  15.2 98.3 %all_to_all.18 = bf16[512,4,128]{0,1,2:T(4,128)(2,1)S(1)} all-to-all(bf16[512,4,128]{0,1,2:T(4,128)(2,1)S(1)} %pad_maximum_fusion), channel_id=1, replica_groups=mesh['band'=4,'row'=64] {'row'}, dimensions={2} | all-to-all | bytes 1048576 | tf_op jit(solution)/shard_map/all_to_all | solution.py:31
  113.4 0.2 copy.16
  113.6 0.4 all_to_all.16
  114.0 0.0 copy-start
  114.0 0.2 slice_convert_fusion.1
  114.2 2.2 %iota_compare_fusion.8 = pred[32768,128]{0,1:T(32,128)(4,1)S(1)} fusion(f32[32768]{0:T(1024)S(1)} %bitcast.37), kind=kLoop, calls=%fused_computation.6.clone.clone.clone.clone.2 | loop fusion | flops 4194304 | bytes 4325376 | tf_op jit(solution)/shard_map/ts,tr->sr/dot_general | solution.py:37
  116.4 4.9 %fusion.6 = bf16[32768,128]{0,1:T(8,128)(2,1)} fusion(f32[32768]{0:T(1024)S(1)} %bitcast.38), kind=kLoop, calls=%fused_computation.8 | loop fusion | flops 8388608 | bytes 8519680 | tf_op jit(solution)/shard_map/convert_element_type | solution.py:36
  121.3 0.0 copy-done
  121.3 14.4 %fusion.50 = pred[32768,128,1,1]{1,0,3,2:T(32,128)(4,1)} fusion(f32[32768]{0:T(1024)S(1)} %bitcast.39), kind=kLoop, calls=%fused_computation.4.clone.clone.clone.clone.clone.clone.2 | loop fusion | flops 4194304 | bytes 4325376 | tf_op jit(solution)/shard_map/ts,tcfr->fcsr/dot_general | solution.py:39
  135.7 0.0 slice-start
  135.7 7.1 %fusion.36 = f32[128,128]{1,0:T(8,128)S(1)} fusion(f32[32768]{0:T(1024)S(1)} %bitcast.40, pred[32768,128]{0,1:T(32,128)(4,1)S(1)} %iota_compare_fusion.8), kind=kOutput, calls=%fused_computation.31 | convolution fusion | flops 1082146816 | bytes 4390912 | tf_op jit(solution)/shard_map/ts,tr->sr/dot_general | solution.py:37
  142.8 0.1 copy.12
  142.9 0.0 slice-done
  143.0 13.1 %fusion.31 = f32[2,2,128,128]{2,3,0,1:T(8,128)S(1)} fusion(bf16[32768,128]{0,1:T(8,128)(2,1)} %fusion.6, bf16[32768,2,2]{0,2,1:T(2,128)(2,1)S(1)} %slice-done, f32[128,128]{0,1:T(8,128)S(1)} %copy.12, pred[32768,128,1,1]{1,0,3,2:T(32,128)(4,1)} %fusion.50), kind=kOutput, calls=%fused_computation.30 | convolution fusion | flops 4311810048 | bytes 13172736 | tf_op jit(solution)/shard_map/ts,tcfr->fcsr/dot_general | solution.py:39
  156.1 0.8 copy.13
  (3 shorter events, 0.0 us)
Async XLA Ops:
  114.0 7.3 %copy-start = (bf16[32768,4,2]{0,2,1:T(2,128)(2,1)}, bf16[32768,4,2]{0,2,1:T(2,128)(2,1)S(1)}, u32[]{:S(2)}) copy-start(bf16[32768,4,2]{0,2,1:T(2,128)(2,1)S(1)} %all_to_all.16) | copy-start | bytes 1572868
  135.7 7.2 %slice-start = ((bf16[32768,4,2]{0,2,1:T(2,128)(2,1)}), bf16[32768,2,2]{0,2,1:T(2,128)(2,1)S(1)}, s32[]{:S(2)}) async-start(bf16[32768,4,2]{0,2,1:T(2,128)(2,1)} %copy-done), calls=%async_computation.1 | async-start | bytes 524288 | tf_op jit(solution)/shard_map/slice | solution.py:32
where the time goes:
time: 157 us
  blocking collectives  98.3 us (63%)
  other arithmetic  32.9 us (21%)
  matrix products  23.7 us (15%)
  local copies, waits for them, and re-layouts  1.89 us (1%)
    all_to_all x1, blocking collectives, local(): lax.all_to_all(packed, 'row', split_axis=2, concat_axis=0, tiled=True)  98.3 us
    dot_general x1, other arithmetic, local(): jnp.einsum('ts,tcfr->fcsr', source_hot, weighted, preferred_element_type=...  14.4 us
    dot_general x1, matrix products, local(): jnp.einsum('ts,tcfr->fcsr', source_hot, weighted, preferred_element_type=...  13.1 us
    another operation x3, other arithmetic  10 us
    dot_general x1, matrix products, local(): jnp.einsum('ts,tr->sr', source_hot, receiver_hot, preferred_element_type=...  7.14 us
    convert_element_type x1, other arithmetic, local(): (receiver_value[:, None] == receiver_range[None, :]).astype(jnp.bfloat16)  4.92 us
    dot_general x1, matrix products, local(): jnp.dot(shot_traces, table, preferred_element_type=jnp.float32)  3.48 us

commit v1 on v0

--- a/solution.py
+++ b/solution.py
@@ -3,10 +3,19 @@
 import jax.numpy as jnp
 from jax import lax
 from jax.sharding import PartitionSpec as P
+from jax.lax import all_to_all, axis_size
 
 FLO = 64
 SC = 128
 RC = 128
+
+
+def move_the_spots(piece_in, chip_axis):
+    base_arr = axis_size(chip_axis)
+    earlier = jnp.split(piece_in, base_arr, axis=2)
+    state_next = jnp.stack(earlier, axis=0)
+    formed = all_to_all(state_next, axis_name=chip_axis, split_axis=0, concat_axis=0)
+    return jnp.concatenate(formed, axis=0)
 
 
 def local(shot_traces, source_cell, receiver_cell, band_order):
@@ -28,7 +37,7 @@
     cells = jnp.stack([source_cell, receiver_cell], axis=1).astype(jnp.bfloat16)
     cells = jnp.broadcast_to(cells[:, :, None], (local_traces, 2, band_size))
     packed = jnp.concatenate([spectra, cells], axis=1)
-    moved = lax.all_to_all(packed, "row", split_axis=2, concat_axis=0, tiled=True)
+    moved = move_the_spots(packed, "row")
     received = moved[:, 0:2, :]
     source_value = moved[:, 2, 0].astype(jnp.float32)
     receiver_value = moved[:, 3, 0].astype(jnp.float32)

time: 157 us -> 158 us (level)
    another operation x3 -> x4, other arithmetic: 10 us -> 10 us
where the time goes in v1:
time: 158 us
  blocking collectives  98.3 us (62%)
  other arithmetic  33.7 us (21%)
  matrix products  23.7 us (15%)
  local copies, waits for them, and re-layouts  1.89 us (1%)
    all_to_all x1, blocking collectives, move_the_spots(): all_to_all(state_next, axis_name=chip_axis, split_axis=0, concat_axis=0)  98.3 us
    dot_general x1, other arithmetic, local(): jnp.einsum('ts,tcfr->fcsr', source_hot, weighted, preferred_element_type=...  14.4 us
    dot_general x1, matrix products, local(): jnp.einsum('ts,tcfr->fcsr', source_hot, weighted, preferred_element_type=...  13.1 us
    another operation x3, other arithmetic  10 us
    dot_general x1, matrix products, local(): jnp.einsum('ts,tr->sr', source_hot, receiver_hot, preferred_element_type=...  7.13 us
    convert_element_type x1, other arithmetic, local(): (receiver_value[:, None] == receiver_range[None, :]).astype(jnp.bfloat16)  4.92 us
    dot_general x1, matrix products, local(): jnp.dot(shot_traces, table, preferred_element_type=jnp.float32)  3.48 us

profile of v1, /device:TPU:44, one launch (start us, length us, event | category | flops | bytes accessed | tf_op | source)
XLA Modules:
  0.0 157.9 jit_solution(200582019703976962)
XLA Ops:
  0.0 0.7 broadcast_add_fusion
  0.7 0.7 convert.18
  1.4 0.7 convert.19
  2.0 8.6 %multiply_convert_fusion.1 = (bf16[4096,128]{1,0:T(8,128)(2,1)S(1)}, bf16[4096,128]{1,0:T(8,128)(2,1)S(1)}) fusion(s32[128]{0:T(128)S(1)} %broadcast_add_fusion), kind=kLoop, calls=%fused_computation.87 | loop fusion | flops 9961472 | bytes 2097664 | tf_op jit(solution)/shard_map/convert.6
  10.7 3.5 %fusion.23 = bf16[256,512]{1,0:T(8,128)(2,1)S(1)} fusion(bf16[512,4096]{1,0:T(8,128)(2,1)} %param.4, bf16[4096,128]{1,0:T(8,128)(2,1)S(1)} %get-tuple-element.8, bf16[4096,128]{1,0:T(8,128)(2,1)S(1)} %get-tuple-element.7), kind=kOutput, calls=%fused_computation.91 | convolution fusion | flops 1078067200 | bytes 6553600 | tf_op jit(solution)/shard_map/dot_general | solution.py:33
  14.2 0.3 copy.72
  14.5 0.1 broadcast_in_dim.2
  16.2 98.3 %all_to_all.5 = bf16[64,512,4,2]{1,2,3,0:T(4,128)(2,1)S(1)} all-to-all(bf16[64,512,4,2]{1,2,3,0:T(4,128)(2,1)S(1)} %constant_dynamic-update-slice_fusion), channel_id=1, replica_groups=mesh['band'=4,'row'=64] {'row'}, dimensions={0} | all-to-all | bytes 1048576 | tf_op jit(solution)/shard_map/all_to_all | solution.py:17
  114.4 0.2 copy.73
  114.6 0.4 reshape.61
  115.0 0.0 copy-start
  115.0 0.2 slice_convert_fusion.1
  115.2 2.2 %iota_compare_fusion.8 = pred[32768,128]{0,1:T(32,128)(4,1)S(1)} fusion(f32[32768]{0:T(1024)S(1)} %bitcast.287), kind=kLoop, calls=%fused_computation.6.clone.clone.clone.clone.2 | loop fusion | flops 4194304 | bytes 4325376 | tf_op jit(solution)/shard_map/ts,tr->sr/dot_general | solution.py:46
  117.4 4.9 %fusion.6 = bf16[32768,128]{0,1:T(8,128)(2,1)} fusion(f32[32768]{0:T(1024)S(1)} %bitcast.288), kind=kLoop, calls=%fused_computation.8 | loop fusion | flops 8388608 | bytes 8519680 | tf_op jit(solution)/shard_map/convert_element_type | solution.py:45
  122.3 0.0 copy-done
  122.3 14.4 %fusion.177 = pred[32768,128,1,1]{1,0,3,2:T(32,128)(4,1)} fusion(f32[32768]{0:T(1024)S(1)} %bitcast.289), kind=kLoop, calls=%fused_computation.4.clone.clone.clone.clone.clone.clone.2 | loop fusion | flops 4194304 | bytes 4325376 | tf_op jit(solution)/shard_map/ts,tcfr->fcsr/dot_general | solution.py:48
  136.7 0.0 slice-start
  136.7 7.1 %fusion.36 = f32[128,128]{1,0:T(8,128)S(1)} fusion(f32[32768]{0:T(1024)S(1)} %bitcast.290, pred[32768,128]{0,1:T(32,128)(4,1)S(1)} %iota_compare_fusion.8), kind=kOutput, calls=%fused_computation.94 | convolution fusion | flops 1082146816 | bytes 4390912 | tf_op jit(solution)/shard_map/ts,tr->sr/dot_general | solution.py:46
  143.8 0.1 copy.74
  143.9 0.0 slice-done
  143.9 13.1 %fusion.31 = f32[2,2,128,128]{2,3,0,1:T(8,128)S(1)} fusion(bf16[32768,128]{0,1:T(8,128)(2,1)} %fusion.6, bf16[32768,2,2]{0,2,1:T(2,128)(2,1)S(1)} %slice-done, f32[128,128]{0,1:T(8,128)S(1)} %copy.74, pred[32768,128,1,1]{1,0,3,2:T(32,128)(4,1)} %fusion.177), kind=kOutput, calls=%fused_computation.93 | convolution fusion | flops 4311810048 | bytes 13172736 | tf_op jit(solution)/shard_map/ts,tcfr->fcsr/dot_general | solution.py:48
  157.0 0.8 copy.75
  (67 shorter events, 1.4 us)
Async XLA Ops:
  115.0 7.3 %copy-start = (bf16[32768,4,2]{0,2,1:T(2,128)(2,1)}, bf16[32768,4,2]{0,2,1:T(2,128)(2,1)S(1)}, u32[]{:S(2)}) copy-start(bf16[32768,4,2]{0,2,1:T(2,128)(2,1)S(1)} %reshape.61) | copy-start | bytes 1572868
  136.7 7.2 %slice-start = ((bf16[32768,4,2]{0,2,1:T(2,128)(2,1)}), bf16[32768,2,2]{0,2,1:T(2,128)(2,1)S(1)}, s32[]{:S(2)}) async-start(bf16[32768,4,2]{0,2,1:T(2,128)(2,1)} %copy-done), calls=%async_computation.1 | async-start | bytes 524288 | tf_op jit(solution)/shard_map/slice | solution.py:41
